TPU v7x, 32 devices: a whole 2x2x4 slice. The times are simulated.
32 devices in a mesh: clip: 2 (over y), tm: 4 (over z), space: 2 (over x), chan: 2 (over core).
Axes of the slice: x: 2, y: 2, z: 4, core: 2. Of those that a mesh axis runs over, the one named last changes fastest.
Arguments:
- features: bfloat16 [16, 8, 90, 256], P(('clip', 'tm'), 'space'), parts along dimension 0, may hold values from -700 to 700
- hidden: bfloat16 [16, 8, 90, 256], P(('clip', 'tm'), 'space'), parts along dimension 0, may hold values from -700 to 700
- cotangent: bfloat16 [16, 8, 90, 256], P(('clip', 'tm'), 'space'), parts along dimension 0, may hold values from -6 to 6
- kernel_one: bfloat16 [256, 3, 3, 3, 256], P(None, None, None, None, 'chan'), may hold values from -0.078125 to 0.078125
- kernel_two: bfloat16 [256, 3, 3, 3, 256], P(None, None, None, None, 'chan'), may hold values from -0.078125 to 0.078125
- gains: float32 [2, 256], replicated, may hold values from 0.25 to 1.75
Outputs:
- feature_grad: bfloat16 [16, 8, 90, 256], P(('clip', 'tm'), 'space', None, 'chan'), parts along dimension 0
- delta_one: float32 [512, 3, 3, 3, 256], P(('clip', 'tm', 'space'), None, None, None, 'chan'), parts along dimension 0
- delta_two: float32 [512, 3, 3, 3, 256], P(('clip', 'tm', 'space'), None, None, None, 'chan'), parts along dimension 0
- gain_grads: float32 [4, 256], P('clip', 'chan'), parts along dimension 0
There are 2 independent parts, one for each index of `clip`. A program takes and returns all parts, laid end to end along the dimension named above; an argument that names none is the same for every part. Nothing has to cross between parts.
All inputs are finite; a program needn't handle non-finite values.
Results may differ from a plain program's by a relative error of at most 0.005.
Values may be sent and summed in bfloat16 or wider, within the bound.
A program may use at most 128 MiB of HBM per device.

v0:
```python
import jax
import jax.numpy as jnp
from jax import lax
from jax.sharding import PartitionSpec as P

GROUPS = 32
epsilon = 1e-06


def extended_2(cells, sides, width):
    for axis, dim in sides:
        count = lax.axis_size(axis)
        ends = count - 1
        head = lax.slice_in_dim(cells, 0, width, axis=dim)
        tail = lax.slice_in_dim(cells, cells.shape[dim] - width, cells.shape[dim], axis=dim)
        cells = jnp.concatenate(
            [
                lax.ppermute(tail, axis, [(i, (i + 1) % count) for i in range(ends)]),
                cells,
                lax.ppermute(head, axis, [((i + 1) % count, i) for i in range(ends)]),
            ],
            axis=dim,
        )
    return cells


def passed_along(block, axis, distance):
    devices = range(lax.axis_size(axis))
    route = [(i - distance, i) for i in devices if i - distance in devices]
    return lax.ppermute(block, axis, route)


def clip_totals(values):
    return lax.psum(values, ("tm", "space"))


def statistics(total, square, members, per):
    mean = jnp.sum(total.reshape(-1, per), axis=1) / members
    spread = jnp.sum(square.reshape(-1, per), axis=1) / members - mean * mean
    scale = lax.rsqrt(spread + epsilon)
    return (jnp.repeat(mean, per), jnp.repeat(scale, per))


def norm_back(upstream, centred, scaled, gain, scale, members, per):
    gate = jax.nn.sigmoid(scaled)
    slope = upstream * gate * (1.0 + scaled * (1.0 - gate))
    totals = clip_totals(
        jnp.stack([jnp.sum(slope, axis=(0, 1, 2)), jnp.sum(slope * centred, axis=(0, 1, 2))])
    )
    first = jnp.repeat(jnp.sum((gain * totals[0]).reshape(-1, per), axis=1), per) / members
    second = jnp.repeat(jnp.sum((gain * totals[1]).reshape(-1, per), axis=1), per) / members
    return (scale * (slope * gain - first - centred * second), totals[1])


def extend(grad):
    edged = extended_2(grad, (("space", 1),), 1)
    later = passed_along(edged, "tm", -1)
    joined = jnp.concatenate([edged, later], axis=0)
    return jnp.pad(joined, ((0, 0), (0, 0), (1, 1), (0, 0)))


def tap_stack(extended, frames, height, width):
    pieces = []
    for frame_tap in range(3):
        for row_tap in range(3):
            for col_tap in range(3):
                pieces.append(
                    extended[
                        2 - frame_tap : 2 - frame_tap + frames,
                        2 - row_tap : 2 - row_tap + height,
                        2 - col_tap : 2 - col_tap + width,
                    ]
                )
    stacked = jnp.stack(pieces, axis=3)
    return stacked.reshape(frames * height * width, 27, extended.shape[3])


def kernel_term(flat_active, taps):
    depth = taps.shape[2]
    flat_taps = taps.reshape(taps.shape[0], 27 * depth)

    def term(start, count):
        product = lax.dot_general(
            flat_active, flat_taps, (((0,), (0,)), ((), ())), preferred_element_type=jnp.float32
        )
        return product.reshape(count, 3, 3, 3, depth)

    return term


def layer_back(active, upstream, kernel, half):
    frames, height, width, channels = active.shape
    taps = tap_stack(extend(upstream), frames, height, width)
    flat_active = active.reshape(frames * height * width, channels)
    term = kernel_term(flat_active, taps)
    partial_grad = lax.dot_general(
        taps,
        kernel.reshape(channels, 27, half),
        (((1, 2), (1, 2)), ((), ())),
        preferred_element_type=jnp.float32,
    )
    back = lax.psum_scatter(
        partial_grad.reshape(frames, height, width, channels),
        "chan",
        scatter_dimension=3,
        tiled=True,
    )
    return (term, back)


def shards(features, hidden, cotangent, kernel_one, kernel_two, gains):
    frames, height, width, channels = features.shape
    half = kernel_one.shape[4]
    per = channels // GROUPS
    offset = lax.axis_index("chan") * half
    members = float(frames * height * width * per * lax.axis_size("tm") * lax.axis_size("space"))
    share = channels // (lax.axis_size("tm") * lax.axis_size("space"))

    def own(field):
        return lax.dynamic_slice_in_dim(field, offset, half, field.ndim - 1)

    field_one = features.astype(jnp.float32)
    field_two = hidden.astype(jnp.float32)
    totals = clip_totals(
        jnp.stack(
            [
                jnp.sum(field_one, axis=(0, 1, 2)),
                jnp.sum(field_one * field_one, axis=(0, 1, 2)),
                jnp.sum(field_two, axis=(0, 1, 2)),
                jnp.sum(field_two * field_two, axis=(0, 1, 2)),
            ]
        )
    )
    mean_one, scale_one = statistics(totals[0], totals[1], members, per)
    mean_two, scale_two = statistics(totals[2], totals[3], members, per)
    centred_one = (field_one - mean_one) * scale_one
    scaled_one = centred_one * gains[0]
    active_one = (scaled_one * jax.nn.sigmoid(scaled_one)).astype(jnp.bfloat16)
    centred_two = (field_two - mean_two) * scale_two
    scaled_two = centred_two * gains[1]
    active_two = (scaled_two * jax.nn.sigmoid(scaled_two)).astype(jnp.bfloat16)
    upstream_two = own(cotangent)
    term_two, back_two = layer_back(active_two, upstream_two, kernel_two, half)
    grad_two, weighted_two = norm_back(
        back_two, own(centred_two), own(scaled_two), own(gains[1]), own(scale_two), members, per
    )
    grad_hidden = grad_two.astype(jnp.bfloat16)
    term_one, back_one = layer_back(active_one, grad_hidden, kernel_one, half)
    start = jnp.int32(0)
    combined = lax.psum_scatter(
        jnp.stack(
            [
                term_one(start, lax.axis_size(("tm", "space")) * share),
                term_two(start, lax.axis_size(("tm", "space")) * share),
            ],
            axis=1,
        ),
        ("tm", "space"),
        scatter_dimension=0,
        tiled=True,
    )
    delta_one = combined[:, 0]
    delta_two = combined[:, 1]
    grad_one, weighted_one = norm_back(
        back_one, own(centred_one), own(scaled_one), own(gains[0]), own(scale_one), members, per
    )
    feature_grad = (own(cotangent).astype(jnp.float32) + grad_one).astype(jnp.bfloat16)
    return (feature_grad, delta_one, delta_two, jnp.stack([weighted_one, weighted_two]))


def solution(mesh):
    placed = (
        P(("clip", "tm"), "space", None, None),
        P(("clip", "tm"), "space", None, None),
        P(("clip", "tm"), "space", None, None),
        P(None, None, None, None, "chan"),
        P(None, None, None, None, "chan"),
        P(),
    )
    return jax.shard_map(
        shards,
        mesh=mesh,
        in_specs=placed,
        out_specs=(
            P(("clip", "tm"), "space", None, "chan"),
            P(("clip", "tm", "space"), None, None, None, "chan"),
            P(("clip", "tm", "space"), None, None, None, "chan"),
            P("clip", "chan"),
        ),
        check_vma=False,
    )
```

profile of v0, /device:TPU:0, one launch (start us, length us, event | category | flops | bytes accessed | tf_op | source)
XLA Modules:
  0.0 289.6 jit_solution(4879320679843734137)
XLA Ops:
  8.4 4.9 %collective-permute-start = (bf16[2,1,90,128]{3,2,1,0:T(8,128)(2,1)S(1)}, bf16[2,1,90,128]{3,2,1,0:T(8,128)(2,1)S(1)}, u32[]{:S(2)}, u32[]{:S(2)}) collective-permute-start(bf16[2,1,90,128]{3,2,1,0:T(8,128)(2,1)S(1)} %get-tuple-element.41), channel_id=1, source_target_pairs={{0,2},{1,3},{4,6},{5,7},{8,10},{9,11},{12,14},{13,15},{16,18},{17,... | collective-permute-start | bytes 138248 | tf_op jit(solution)/shard_map/ppermute | solution.py:18
  15.1 4.2 %collective-permute-done.1 = bf16[2,1,90,128]{3,2,1,0:T(8,128)(2,1)S(1)} collective-permute-done((bf16[2,1,90,128]{3,2,1,0:T(8,128)(2,1)S(1)}, bf16[2,1,90,128]{3,2,1,0:T(8,128)(2,1)S(1)}, u32[]{:S(2)}, u32[]{:S(2)}) %collective-permute-start.1) | collective-permute-done | bytes 46112 | tf_op jit(solution)/shard_map/ppermute | solution.py:20
  20.6 7.9 %collective-permute-done.2 = bf16[2,6,90,128]{3,2,1,0:T(8,128)(2,1)S(1)} collective-permute-done((bf16[2,6,90,128]{3,2,1,0:T(8,128)(2,1)S(1)}, bf16[2,6,90,128]{3,2,1,0:T(8,128)(2,1)S(1)}, u32[]{:S(2)}, u32[]{:S(2)}) %collective-permute-start.2) | collective-permute-done | bytes 276512 | tf_op jit(solution)/shard_map/ppermute | solution.py:30
  30.3 2.3 copy-done.3
  32.7 2.5 convolution_bitcast_fusion.2
  35.6 18.1 %psum.21 = f32[4,256]{1,0:T(4,128)S(1)} all-reduce(f32[4,256]{1,0:T(4,128)S(1)} %pad_maximum_fusion.8), channel_id=1, replica_groups=mesh['clip'=2,'tm'=4,'space'=2,'chan'=2] {'tm','space'}, use_global_device_ids=true, to_apply=%region_4.0 | all-reduce | flops 1024 | bytes 8192 | tf_op jit(solution)/shard_map/psum | solution.py:34
  56.8 18.2 %psum.22 = f32[2,128]{1,0:T(2,128)S(1)} all-reduce(f32[2,128]{1,0:T(2,128)S(1)} %pad_maximum_fusion.9), channel_id=1, replica_groups=mesh['clip'=2,'tm'=4,'space'=2,'chan'=2] {'tm','space'}, use_global_device_ids=true, to_apply=%region_12.13 | all-reduce | flops 256 | bytes 2048 | tf_op jit(solution)/shard_map/psum | solution.py:34
  75.9 2.9 collective-permute-start.3
  80.5 4.3 %collective-permute-done.4 = bf16[2,1,90,128]{3,2,1,0:T(8,128)(2,1)S(1)} collective-permute-done((bf16[2,1,90,128]{3,2,1,0:T(8,128)(2,1)S(1)}, bf16[2,1,90,128]{3,2,1,0:T(8,128)(2,1)S(1)}, u32[]{:S(2)}, u32[]{:S(2)}) %collective-permute-start.4) | collective-permute-done | bytes 46112 | tf_op jit(solution)/shard_map/ppermute | solution.py:20
  86.9 6.5 %collective-permute-done.5 = bf16[2,6,90,128]{3,2,1,0:T(8,128)(2,1)S(1)} collective-permute-done((bf16[2,6,90,128]{3,2,1,0:T(8,128)(2,1)S(1)}, bf16[2,6,90,128]{3,2,1,0:T(8,128)(2,1)S(1)}, u32[]{:S(2)}, u32[]{:S(2)}) %collective-permute-start.5) | collective-permute-done | bytes 276512 | tf_op jit(solution)/shard_map/ppermute | solution.py:30
  95.6 1.6 fusion
  99.3 4.6 %copy.72 = bf16[2,4,90,27,128]{4,3,2,1,0:T(8,128)(2,1)S(1)} copy(bf16[2,4,90,27,128]{4,2,3,1,0:T(8,128)(2,1)} %copy-done.3) | data formatting | bytes 9953280 | tf_op jit(solution)/shard_map/stack | solution.py:74
  103.9 7.3 %copy.111 = bf16[90,8,27,128]{3,1,2,0:T(8,128)(2,1)} copy(bf16[90,8,27,128]{3,2,1,0:T(8,128)(2,1)S(1)} %bitcast.258) | data formatting | bytes 9953280
  111.2 7.9 %copy.73 = bf16[3456,720]{1,0:T(8,128)(2,1)} copy(bf16[3456,720]{0,1:T(8,128)(2,1)} %bitcast.262) | data formatting | bytes 9953280 | tf_op jit(solution)/shard_map/dot_general | solution.py:83
  119.1 6.0 %convolution_bitcast_fusion = f32[256,1,3,3,3,128]{5,0,4,3,2,1:T(8,128)} fusion(bf16[3,3,3,128,720]{4,3,2,1,0:T(8,128)(2,1)} %bitcast.260, bf16[720,256,1,1,1]{1,0,2,3,4:T(8,128)(2,1)S(1)} %reshape.335), kind=kOutput, calls=%fused_computation.5 | convolution fusion | flops 1274019840 | bytes 8884224 | tf_op jit(solution)/shard_map/dot_general | solution.py:83
  125.1 5.8 %copy.69 = bf16[2,4,90,27,128]{4,3,2,1,0:T(8,128)(2,1)S(1)} copy(bf16[2,4,90,27,128]{4,2,1,0,3:T(8,128)(2,1)} %copy-done.4) | data formatting | bytes 9953280 | tf_op jit(solution)/shard_map/stack | solution.py:74
  130.9 7.3 %copy.112 = bf16[90,8,27,128]{3,1,2,0:T(8,128)(2,1)} copy(bf16[90,8,27,128]{3,2,1,0:T(8,128)(2,1)S(1)} %bitcast.259) | data formatting | bytes 9953280
  138.2 8.0 %copy.70 = bf16[3456,720]{1,0:T(8,128)(2,1)} copy(bf16[3456,720]{0,1:T(8,128)(2,1)} %bitcast.263) | data formatting | bytes 9953280 | tf_op jit(solution)/shard_map/dot_general | solution.py:83
  146.2 4.3 %convolution_bitcast_fusion.1 = f32[256,1,3,3,3,128]{5,0,4,3,2,1:T(8,128)S(1)} fusion(bf16[3,3,3,128,720]{4,3,2,1,0:T(8,128)(2,1)} %bitcast.261, bf16[720,256,1,1,1]{1,0,2,3,4:T(8,128)(2,1)S(1)} %reshape.334), kind=kOutput, calls=%fused_computation.6 | convolution fusion | flops 1274019840 | bytes 8884224 | tf_op jit(solution)/shard_map/dot_general | solution.py:83
  150.5 3.4 %pad_maximum_fusion = f32[256,2,3,3,3,128]{5,0,4,3,2,1:T(8,128)} fusion(f32[256,1,3,3,3,128]{5,0,4,3,2,1:T(8,128)S(1)} %copy-done.2, f32[256,1,3,3,3,128]{5,0,4,3,2,1:T(8,128)S(1)} %convolution_bitcast_fusion.1), kind=kLoop, calls=%fused_computation | loop fusion | flops 1769472 | bytes 14155776 | tf_op jit(solution)/shard_map/stack | solution.py:151
  154.0 2.0 fusion.36
  156.0 18.2 %psum.23 = f32[2,128]{1,0:T(2,128)S(1)} all-reduce(f32[2,128]{1,0:T(2,128)S(1)} %pad_maximum_fusion.10), channel_id=1, replica_groups=mesh['clip'=2,'tm'=4,'space'=2,'chan'=2] {'tm','space'}, use_global_device_ids=true, to_apply=%region_18.19 | all-reduce | flops 256 | bytes 2048 | tf_op jit(solution)/shard_map/psum | solution.py:34
  177.5 103.5 %reduce-scatter.8.cloned.1.call-done = f32[32,2,3,3,3,128]{5,0,4,3,2,1:T(8,128)} async-done(((f32[256,2,3,3,3,128]{5,0,4,3,2,1:T(8,128)}), f32[32,2,3,3,3,128]{5,0,4,3,2,1:T(8,128)}) %reduce-scatter.8.cloned.1.call-update) | async-done | bytes 884752 | tf_op jit(solution)/shard_map/reduce_scatter | solution.py:150
  281.0 2.1 slice_bitcast_fusion
  (158 shorter events, 21.5 us)
Async XLA Ops:
  7.2 23.1 %copy-start = (bf16[256,3,3,3,128]{4,0,3,2,1:T(8,128)(2,1)S(1)}, bf16[256,3,3,3,128]{4,0,3,2,1:T(8,128)(2,1)}, u32[]{:S(2)}) copy-start(bf16[256,3,3,3,128]{4,0,3,2,1:T(8,128)(2,1)} %param.10) | copy-start | bytes 5308420
  7.2 48.4 %reduce-scatter.4.cloned.1.call-start = ((), (), s32[]{:S(2)}) async-start(), calls=%async_computation.3 | async-start | bytes 1179648 | tf_op jit(solution)/shard_map/reduce_scatter | solution.py:102
  8.4 6.6 %collective-permute-start = (bf16[2,1,90,128]{3,2,1,0:T(8,128)(2,1)S(1)}, bf16[2,1,90,128]{3,2,1,0:T(8,128)(2,1)S(1)}, u32[]{:S(2)}, u32[]{:S(2)}) collective-permute-start(bf16[2,1,90,128]{3,2,1,0:T(8,128)(2,1)S(1)} %get-tuple-element.41), channel_id=1, source_target_pairs={{0,2},{1,3},{4,6},{5,7},{8,10},{9,11},{12,14},{13,15},{16,18},{17,... | collective-permute-start | bytes 138248 | tf_op jit(solution)/shard_map/ppermute | solution.py:18
  13.3 6.0 %collective-permute-start.1 = (bf16[2,1,90,128]{3,2,1,0:T(8,128)(2,1)S(1)}, bf16[2,1,90,128]{3,2,1,0:T(8,128)(2,1)S(1)}, u32[]{:S(2)}, u32[]{:S(2)}) collective-permute-start(bf16[2,1,90,128]{3,2,1,0:T(8,128)(2,1)S(1)} %get-tuple-element.40), channel_id=1, source_target_pairs={{2,0},{3,1},{6,4},{7,5},{10,8},{11,9},{14,12},{15,13},{18,16},{19,... | collective-permute-start | bytes 138248 | tf_op jit(solution)/shard_map/ppermute | solution.py:20
  19.3 9.2 %collective-permute-start.2 = (bf16[2,6,90,128]{3,2,1,0:T(8,128)(2,1)S(1)}, bf16[2,6,90,128]{3,2,1,0:T(8,128)(2,1)S(1)}, u32[]{:S(2)}, u32[]{:S(2)}) collective-permute-start(bf16[2,6,90,128]{3,2,1,0:T(8,128)(2,1)S(1)} %constant_dynamic-update-slice_fusion), channel_id=1, source_target_pairs={{4,0},{8,4},{12,8},{5,1},{9,5},{13,9},{6,2},{10,6},{14,10},{7,3},{... | collective-permute-start | bytes 829448 | tf_op jit(solution)/shard_map/ppermute | solution.py:30
  30.3 2.3 copy-start.3
  30.3 4.9 %copy-start.7 = (bf16[2,4,90,256]{3,1,2,0:T(4,128)(2,1)S(1)}, bf16[2,4,90,256]{3,1,2,0:T(4,128)(2,1)}, u32[]{:S(2)}) copy-start(bf16[2,4,90,256]{3,1,2,0:T(4,128)(2,1)} %param.6) | copy-start | bytes 1105924
  32.7 2.7 copy-start.6
  32.7 21.9 %copy-start.9 = (f32[2,256]{1,0:T(2,128)S(1)}, f32[2,256]{1,0:T(2,128)}, u32[]{:S(2)}) copy-start(f32[2,256]{1,0:T(2,128)} %param.11) | copy-start | bytes 6148
  35.2 118.8 %reduce-scatter.6.cloned.1.call-start = ((), (), s32[]{:S(2)}) async-start(), calls=%async_computation.4 | async-start | bytes 1179648 | tf_op jit(solution)/shard_map/reduce_scatter | solution.py:102
  75.9 4.6 %collective-permute-start.3 = (bf16[2,1,90,128]{3,2,1,0:T(8,128)(2,1)S(1)}, bf16[2,1,90,128]{3,2,1,0:T(8,128)(2,1)S(1)}, u32[]{:S(2)}, u32[]{:S(2)}) collective-permute-start(bf16[2,1,90,128]{3,2,1,0:T(8,128)(2,1)S(1)} %get-tuple-element.38), channel_id=1, source_target_pairs={{0,2},{1,3},{4,6},{5,7},{8,10},{9,11},{12,14},{13,15},{16,18},{17,... | collective-permute-start | bytes 138248 | tf_op jit(solution)/shard_map/ppermute | solution.py:18
  78.8 6.0 %collective-permute-start.4 = (bf16[2,1,90,128]{3,2,1,0:T(8,128)(2,1)S(1)}, bf16[2,1,90,128]{3,2,1,0:T(8,128)(2,1)S(1)}, u32[]{:S(2)}, u32[]{:S(2)}) collective-permute-start(bf16[2,1,90,128]{3,2,1,0:T(8,128)(2,1)S(1)} %get-tuple-element.39), channel_id=1, source_target_pairs={{2,0},{3,1},{6,4},{7,5},{10,8},{11,9},{14,12},{15,13},{18,16},{19,... | collective-permute-start | bytes 138248 | tf_op jit(solution)/shard_map/ppermute | solution.py:20
  84.8 8.6 %collective-permute-start.5 = (bf16[2,6,90,128]{3,2,1,0:T(8,128)(2,1)S(1)}, bf16[2,6,90,128]{3,2,1,0:T(8,128)(2,1)S(1)}, u32[]{:S(2)}, u32[]{:S(2)}) collective-permute-start(bf16[2,6,90,128]{3,2,1,0:T(8,128)(2,1)S(1)} %pad_maximum_fusion.3), channel_id=1, source_target_pairs={{4,0},{8,4},{12,8},{5,1},{9,5},{13,9},{6,2},{10,6},{14,10},{7,3},{... | collective-permute-start | bytes 829448 | tf_op jit(solution)/shard_map/ppermute | solution.py:30
  94.2 1.5 copy-start.10
  95.2 2.3 copy-start.4
  95.6 3.1 %copy-start.8 = (bf16[2,4,90,256]{3,1,2,0:T(4,128)(2,1)S(1)}, bf16[2,4,90,256]{3,1,2,0:T(4,128)(2,1)}, u32[]{:S(2)}) copy-start(bf16[2,4,90,256]{3,1,2,0:T(4,128)(2,1)} %param.6) | copy-start | bytes 1105924
  97.5 1.6 copy-start.5
  98.5 182.5 %reduce-scatter.8.cloned.1.call-start = ((), (), s32[]{:S(2)}) async-start(), calls=%async_computation.5 | async-start | bytes 7962624 | tf_op jit(solution)/shard_map/reduce_scatter | solution.py:150
  146.2 4.3 %copy-start.2 = (f32[256,1,3,3,3,128]{5,0,4,3,2,1:T(8,128)S(1)}, f32[256,1,3,3,3,128]{5,0,4,3,2,1:T(8,128)}, u32[]{:S(2)}) copy-start(f32[256,1,3,3,3,128]{5,0,4,3,2,1:T(8,128)} %convolution_bitcast_fusion) | copy-start | bytes 10616836
  153.9 129.2 %copy-start.1 = (bf16[256,3,3,3,128]{4,0,3,2,1:T(8,128)(2,1)S(1)}, bf16[256,3,3,3,128]{4,0,3,2,1:T(8,128)(2,1)}, u32[]{:S(2)}) copy-start(bf16[256,3,3,3,128]{4,0,3,2,1:T(8,128)(2,1)} %param.10) | copy-start | bytes 5308420
Sparse Core Ops, SparseCore 0:
  35.3 7.4 reduce-scatter.3
  98.6 5.4 reduce-scatter.5
  154.0 126.9 reduce-scatter.7
where the time goes:
time: 291 us; the launch traced here: 290 us
  waiting for transfers between devices  127 us (44%)
  blocking collectives  54.5 us (19%)
  local copies, waits for them, and re-layouts  54.4 us (19%)
  matrix products  14.5 us (5%)
  between operations  14.3 us (5%)
  starting transfers between devices  13.2 us (5%)
  other arithmetic  11.5 us (4%)
    reduce_scatter x1, waiting for transfers between devices, shards(): lax.psum_scatter(jnp.stack([term_one(start, lax.axis_size(('tm', 'space')...  104 us
    psum x3, blocking collectives, clip_totals(): return lax.psum(values, ('tm', 'space'))  54.5 us
    unnamed x73, local copies, waits for them, and re-layouts  21.3 us
    dot_general x2, local copies, waits for them, and re-layouts, term(): lax.dot_general(flat_active, flat_taps, (((0,), (0,)), ((), ())), preferr...  15.9 us
    ppermute x2, waiting for transfers between devices, passed_along(): return lax.ppermute(block, axis, route)  14.5 us
    another operation x4, local copies, waits for them, and re-layouts, tap_stack(): stacked = jnp.stack(pieces, axis=3)  10.6 us
    dot_general x2, matrix products, term(): lax.dot_general(flat_active, flat_taps, (((0,), (0,)), ((), ())), preferr...  10.3 us
    ppermute x2, waiting for transfers between devices, extended_2(): lax.ppermute(head, axis, [((i + 1) % count, i) for i in range(ends)])  8.45 us
  transfers between devices with their start and end apart: 9, of which 7 were waited for; matrix products, arithmetic and copies ran while one was open for 22% of the time, Pallas kernels for 0%

commit v1 on v0

--- a/solution.py
+++ b/solution.py
@@ -5,6 +5,9 @@
 
 GROUPS = 32
 epsilon = 1e-06
+clusters_replace = lambda block_here: jnp.sum(
+    jax.lax.all_gather(block_here, ("tm", "space")), axis=0
+)
 
 
 def extended_2(cells, sides, width):
@@ -31,7 +34,7 @@
 
 
 def clip_totals(values):
-    return lax.psum(values, ("tm", "space"))
+    return clusters_replace(values)
 
 
 def statistics(total, square, members, per):

time: 291 us -> 302 us (1.038)
  blocking collectives: 54.5 us -> 64.7 us
    all_gather x0 -> x3, blocking collectives: none -> 64.7 us  [jax.lax.all_gather(block_here, ('tm', 'space'))]
    psum x3 -> x0, blocking collectives: 54.5 us -> none  [clip_totals(): return lax.psum(values, ('tm', 'space'))]
  transfers between devices with their start and end apart: 9 -> 9, of which waited for: 7 -> 7; matrix products, arithmetic and copies ran while one was open for 22% -> 21% of each run, Pallas kernels for 0% -> 0%
where the time goes in v1:
time: 302 us; the launch traced here: 301 us
  waiting for transfers between devices  129 us (43%)
  blocking collectives  64.7 us (21%)
  local copies, waits for them, and re-layouts  54.4 us (18%)
  matrix products  14.5 us (5%)
  between operations  14.3 us (5%)
  starting transfers between devices  13.3 us (4%)
  other arithmetic  11.5 us (4%)
    reduce_scatter x1, waiting for transfers between devices, shards(): lax.psum_scatter(jnp.stack([term_one(start, lax.axis_size(('tm', 'space')...  105 us
    all_gather x3, blocking collectives, jax.lax.all_gather(block_here, ('tm', 'space'))  64.7 us
    unnamed x73, local copies, waits for them, and re-layouts  21.3 us
    dot_general x2, local copies, waits for them, and re-layouts, term(): lax.dot_general(flat_active, flat_taps, (((0,), (0,)), ((), ())), preferr...  15.9 us
    ppermute x2, waiting for transfers between devices, passed_along(): return lax.ppermute(block, axis, route)  14.5 us
    another operation x4, local copies, waits for them, and re-layouts, tap_stack(): stacked = jnp.stack(pieces, axis=3)  10.6 us
    dot_general x2, matrix products, term(): lax.dot_general(flat_active, flat_taps, (((0,), (0,)), ((), ())), preferr...  10.3 us
    ppermute x2, waiting for transfers between devices, extended_2(): lax.ppermute(head, axis, [((i + 1) % count, i) for i in range(ends)])  8.45 us
  transfers between devices with their start and end apart: 9, of which 7 were waited for; matrix products, arithmetic and copies ran while one was open for 21% of the time, Pallas kernels for 0%

profile of v1, /device:TPU:0, one launch (start us, length us, event | category | flops | bytes accessed | tf_op | source)
XLA Modules:
  0.0 301.2 jit_solution(11042020559190191468)
XLA Ops:
  8.4 4.9 %collective-permute-start = (bf16[2,1,90,128]{3,2,1,0:T(8,128)(2,1)S(1)}, bf16[2,1,90,128]{3,2,1,0:T(8,128)(2,1)S(1)}, u32[]{:S(2)}, u32[]{:S(2)}) collective-permute-start(bf16[2,1,90,128]{3,2,1,0:T(8,128)(2,1)S(1)} %get-tuple-element.45), channel_id=1, source_target_pairs={{0,2},{1,3},{4,6},{5,7},{8,10},{9,11},{12,14},{13,15},{16,18},{17,... | collective-permute-start | bytes 138248 | tf_op jit(solution)/shard_map/ppermute | solution.py:21
  15.1 4.2 %collective-permute-done.1 = bf16[2,1,90,128]{3,2,1,0:T(8,128)(2,1)S(1)} collective-permute-done((bf16[2,1,90,128]{3,2,1,0:T(8,128)(2,1)S(1)}, bf16[2,1,90,128]{3,2,1,0:T(8,128)(2,1)S(1)}, u32[]{:S(2)}, u32[]{:S(2)}) %collective-permute-start.1) | collective-permute-done | bytes 46112 | tf_op jit(solution)/shard_map/ppermute | solution.py:23
  20.6 7.9 %collective-permute-done.2 = bf16[2,6,90,128]{3,2,1,0:T(8,128)(2,1)S(1)} collective-permute-done((bf16[2,6,90,128]{3,2,1,0:T(8,128)(2,1)S(1)}, bf16[2,6,90,128]{3,2,1,0:T(8,128)(2,1)S(1)}, u32[]{:S(2)}, u32[]{:S(2)}) %collective-permute-start.2) | collective-permute-done | bytes 276512 | tf_op jit(solution)/shard_map/ppermute | solution.py:33
  30.3 2.3 copy-done.3
  32.7 2.5 convolution_bitcast_fusion.2
  35.6 30.6 %all-gather.3 = f32[8,4,256]{2,1,0:T(4,128)S(1)} all-gather(f32[1,4,256]{2,1,0:T(4,128)S(1)} %maximum_bitcast_fusion), channel_id=2, replica_groups=mesh['clip'=2,'tm'=4,'space'=2,'chan'=2] {'tm','space'}, dimensions={0}, use_global_device_ids=true | all-gather | bytes 36864 | tf_op jit(solution)/shard_map/all_gather | solution.py:9
  69.3 17.3 %all-gather.4 = f32[8,2,128]{2,1,0:T(2,128)S(1)} all-gather(f32[1,2,128]{2,1,0:T(2,128)S(1)} %maximum_bitcast_fusion.1), channel_id=3, replica_groups=mesh['clip'=2,'tm'=4,'space'=2,'chan'=2] {'tm','space'}, dimensions={0}, use_global_device_ids=true | all-gather | bytes 9216 | tf_op jit(solution)/shard_map/all_gather | solution.py:9
  87.5 2.9 collective-permute-start.3
  92.2 4.3 %collective-permute-done.4 = bf16[2,1,90,128]{3,2,1,0:T(8,128)(2,1)S(1)} collective-permute-done((bf16[2,1,90,128]{3,2,1,0:T(8,128)(2,1)S(1)}, bf16[2,1,90,128]{3,2,1,0:T(8,128)(2,1)S(1)}, u32[]{:S(2)}, u32[]{:S(2)}) %collective-permute-start.4) | collective-permute-done | bytes 46112 | tf_op jit(solution)/shard_map/ppermute | solution.py:23
  98.6 6.6 %collective-permute-done.5 = bf16[2,6,90,128]{3,2,1,0:T(8,128)(2,1)S(1)} collective-permute-done((bf16[2,6,90,128]{3,2,1,0:T(8,128)(2,1)S(1)}, bf16[2,6,90,128]{3,2,1,0:T(8,128)(2,1)S(1)}, u32[]{:S(2)}, u32[]{:S(2)}) %collective-permute-start.5) | collective-permute-done | bytes 276512 | tf_op jit(solution)/shard_map/ppermute | solution.py:33
  107.4 1.6 fusion.2
  111.0 4.6 %copy.109 = bf16[2,4,90,27,128]{4,3,2,1,0:T(8,128)(2,1)S(1)} copy(bf16[2,4,90,27,128]{4,2,3,1,0:T(8,128)(2,1)} %copy-done.3) | data formatting | bytes 9953280 | tf_op jit(solution)/shard_map/stack | solution.py:77
  115.6 7.3 %copy.146 = bf16[90,8,27,128]{3,1,2,0:T(8,128)(2,1)} copy(bf16[90,8,27,128]{3,2,1,0:T(8,128)(2,1)S(1)} %bitcast.263) | data formatting | bytes 9953280
  122.9 7.9 %copy.110 = bf16[3456,720]{1,0:T(8,128)(2,1)} copy(bf16[3456,720]{0,1:T(8,128)(2,1)} %bitcast.267) | data formatting | bytes 9953280 | tf_op jit(solution)/shard_map/dot_general | solution.py:86
  130.8 6.0 %convolution_bitcast_fusion = f32[256,1,3,3,3,128]{5,0,4,3,2,1:T(8,128)} fusion(bf16[3,3,3,128,720]{4,3,2,1,0:T(8,128)(2,1)} %bitcast.265, bf16[720,256,1,1,1]{1,0,2,3,4:T(8,128)(2,1)S(1)} %reshape.347), kind=kOutput, calls=%fused_computation.5 | convolution fusion | flops 1274019840 | bytes 8884224 | tf_op jit(solution)/shard_map/dot_general | solution.py:86
  136.8 5.8 %copy.106 = bf16[2,4,90,27,128]{4,3,2,1,0:T(8,128)(2,1)S(1)} copy(bf16[2,4,90,27,128]{4,2,1,0,3:T(8,128)(2,1)} %copy-done.4) | data formatting | bytes 9953280 | tf_op jit(solution)/shard_map/stack | solution.py:77
  142.6 7.3 %copy.147 = bf16[90,8,27,128]{3,1,2,0:T(8,128)(2,1)} copy(bf16[90,8,27,128]{3,2,1,0:T(8,128)(2,1)S(1)} %bitcast.264) | data formatting | bytes 9953280
  149.9 8.0 %copy.107 = bf16[3456,720]{1,0:T(8,128)(2,1)} copy(bf16[3456,720]{0,1:T(8,128)(2,1)} %bitcast.268) | data formatting | bytes 9953280 | tf_op jit(solution)/shard_map/dot_general | solution.py:86
  157.9 4.3 %convolution_bitcast_fusion.1 = f32[256,1,3,3,3,128]{5,0,4,3,2,1:T(8,128)S(1)} fusion(bf16[3,3,3,128,720]{4,3,2,1,0:T(8,128)(2,1)} %bitcast.266, bf16[720,256,1,1,1]{1,0,2,3,4:T(8,128)(2,1)S(1)} %reshape.346), kind=kOutput, calls=%fused_computation.6 | convolution fusion | flops 1274019840 | bytes 8884224 | tf_op jit(solution)/shard_map/dot_general | solution.py:86
  162.2 3.4 %pad_maximum_fusion = f32[256,2,3,3,3,128]{5,0,4,3,2,1:T(8,128)} fusion(f32[256,1,3,3,3,128]{5,0,4,3,2,1:T(8,128)S(1)} %copy-done.2, f32[256,1,3,3,3,128]{5,0,4,3,2,1:T(8,128)S(1)} %convolution_bitcast_fusion.1), kind=kLoop, calls=%fused_computation | loop fusion | flops 1769472 | bytes 14155776 | tf_op jit(solution)/shard_map/stack | solution.py:154
  165.7 2.0 fusion.39
  167.7 16.8 %all-gather.5 = f32[8,2,128]{2,1,0:T(2,128)S(1)} all-gather(f32[1,2,128]{2,1,0:T(2,128)S(1)} %maximum_bitcast_fusion.2), channel_id=4, replica_groups=mesh['clip'=2,'tm'=4,'space'=2,'chan'=2] {'tm','space'}, dimensions={0}, use_global_device_ids=true | all-gather | bytes 9216 | tf_op jit(solution)/shard_map/all_gather | solution.py:9
  187.8 104.8 %reduce-scatter.8.cloned.1.call-done = f32[32,2,3,3,3,128]{5,0,4,3,2,1:T(8,128)} async-done(((f32[256,2,3,3,3,128]{5,0,4,3,2,1:T(8,128)}), f32[32,2,3,3,3,128]{5,0,4,3,2,1:T(8,128)}) %reduce-scatter.8.cloned.1.call-update) | async-done | bytes 884752 | tf_op jit(solution)/shard_map/reduce_scatter | solution.py:153
  292.6 2.1 slice_bitcast_fusion
  (161 shorter events, 21.6 us)
Async XLA Ops:
  7.2 23.1 %copy-start = (bf16[256,3,3,3,128]{4,0,3,2,1:T(8,128)(2,1)S(1)}, bf16[256,3,3,3,128]{4,0,3,2,1:T(8,128)(2,1)}, u32[]{:S(2)}) copy-start(bf16[256,3,3,3,128]{4,0,3,2,1:T(8,128)(2,1)} %param.10) | copy-start | bytes 5308420
  7.2 60.9 %reduce-scatter.4.cloned.1.call-start = ((), (), s32[]{:S(2)}) async-start(), calls=%async_computation.3 | async-start | bytes 1179648 | tf_op jit(solution)/shard_map/reduce_scatter | solution.py:105
  8.4 6.6 %collective-permute-start = (bf16[2,1,90,128]{3,2,1,0:T(8,128)(2,1)S(1)}, bf16[2,1,90,128]{3,2,1,0:T(8,128)(2,1)S(1)}, u32[]{:S(2)}, u32[]{:S(2)}) collective-permute-start(bf16[2,1,90,128]{3,2,1,0:T(8,128)(2,1)S(1)} %get-tuple-element.45), channel_id=1, source_target_pairs={{0,2},{1,3},{4,6},{5,7},{8,10},{9,11},{12,14},{13,15},{16,18},{17,... | collective-permute-start | bytes 138248 | tf_op jit(solution)/shard_map/ppermute | solution.py:21
  13.3 6.0 %collective-permute-start.1 = (bf16[2,1,90,128]{3,2,1,0:T(8,128)(2,1)S(1)}, bf16[2,1,90,128]{3,2,1,0:T(8,128)(2,1)S(1)}, u32[]{:S(2)}, u32[]{:S(2)}) collective-permute-start(bf16[2,1,90,128]{3,2,1,0:T(8,128)(2,1)S(1)} %get-tuple-element.44), channel_id=1, source_target_pairs={{2,0},{3,1},{6,4},{7,5},{10,8},{11,9},{14,12},{15,13},{18,16},{19,... | collective-permute-start | bytes 138248 | tf_op jit(solution)/shard_map/ppermute | solution.py:23
  19.3 9.2 %collective-permute-start.2 = (bf16[2,6,90,128]{3,2,1,0:T(8,128)(2,1)S(1)}, bf16[2,6,90,128]{3,2,1,0:T(8,128)(2,1)S(1)}, u32[]{:S(2)}, u32[]{:S(2)}) collective-permute-start(bf16[2,6,90,128]{3,2,1,0:T(8,128)(2,1)S(1)} %constant_dynamic-update-slice_fusion), channel_id=1, source_target_pairs={{4,0},{8,4},{12,8},{5,1},{9,5},{13,9},{6,2},{10,6},{14,10},{7,3},{... | collective-permute-start | bytes 829448 | tf_op jit(solution)/shard_map/ppermute | solution.py:33
  30.3 2.3 copy-start.3
  30.3 4.9 %copy-start.7 = (bf16[2,4,90,256]{3,1,2,0:T(4,128)(2,1)S(1)}, bf16[2,4,90,256]{3,1,2,0:T(4,128)(2,1)}, u32[]{:S(2)}) copy-start(bf16[2,4,90,256]{3,1,2,0:T(4,128)(2,1)} %param.6) | copy-start | bytes 1105924
  32.7 2.7 copy-start.6
  32.7 34.4 %copy-start.9 = (f32[2,256]{1,0:T(2,128)S(1)}, f32[2,256]{1,0:T(2,128)}, u32[]{:S(2)}) copy-start(f32[2,256]{1,0:T(2,128)} %param.11) | copy-start | bytes 6148
  35.2 130.5 %reduce-scatter.6.cloned.1.call-start = ((), (), s32[]{:S(2)}) async-start(), calls=%async_computation.4 | async-start | bytes 1179648 | tf_op jit(solution)/shard_map/reduce_scatter | solution.py:105
  87.5 4.7 %collective-permute-start.3 = (bf16[2,1,90,128]{3,2,1,0:T(8,128)(2,1)S(1)}, bf16[2,1,90,128]{3,2,1,0:T(8,128)(2,1)S(1)}, u32[]{:S(2)}, u32[]{:S(2)}) collective-permute-start(bf16[2,1,90,128]{3,2,1,0:T(8,128)(2,1)S(1)} %get-tuple-element.42), channel_id=1, source_target_pairs={{0,2},{1,3},{4,6},{5,7},{8,10},{9,11},{12,14},{13,15},{16,18},{17,... | collective-permute-start | bytes 138248 | tf_op jit(solution)/shard_map/ppermute | solution.py:21
  90.5 6.0 %collective-permute-start.4 = (bf16[2,1,90,128]{3,2,1,0:T(8,128)(2,1)S(1)}, bf16[2,1,90,128]{3,2,1,0:T(8,128)(2,1)S(1)}, u32[]{:S(2)}, u32[]{:S(2)}) collective-permute-start(bf16[2,1,90,128]{3,2,1,0:T(8,128)(2,1)S(1)} %get-tuple-element.43), channel_id=1, source_target_pairs={{2,0},{3,1},{6,4},{7,5},{10,8},{11,9},{14,12},{15,13},{18,16},{19,... | collective-permute-start | bytes 138248 | tf_op jit(solution)/shard_map/ppermute | solution.py:23
  96.5 8.6 %collective-permute-start.5 = (bf16[2,6,90,128]{3,2,1,0:T(8,128)(2,1)S(1)}, bf16[2,6,90,128]{3,2,1,0:T(8,128)(2,1)S(1)}, u32[]{:S(2)}, u32[]{:S(2)}) collective-permute-start(bf16[2,6,90,128]{3,2,1,0:T(8,128)(2,1)S(1)} %pad_maximum_fusion.3), channel_id=1, source_target_pairs={{4,0},{8,4},{12,8},{5,1},{9,5},{13,9},{6,2},{10,6},{14,10},{7,3},{... | collective-permute-start | bytes 829448 | tf_op jit(solution)/shard_map/ppermute | solution.py:33
  105.9 1.5 copy-start.10
  106.9 2.3 copy-start.4
  107.4 3.1 %copy-start.8 = (bf16[2,4,90,256]{3,1,2,0:T(4,128)(2,1)S(1)}, bf16[2,4,90,256]{3,1,2,0:T(4,128)(2,1)}, u32[]{:S(2)}) copy-start(bf16[2,4,90,256]{3,1,2,0:T(4,128)(2,1)} %param.6) | copy-start | bytes 1105924
  109.2 1.6 copy-start.5
  110.2 182.4 %reduce-scatter.8.cloned.1.call-start = ((), (), s32[]{:S(2)}) async-start(), calls=%async_computation.5 | async-start | bytes 7962624 | tf_op jit(solution)/shard_map/reduce_scatter | solution.py:153
  157.9 4.3 %copy-start.2 = (f32[256,1,3,3,3,128]{5,0,4,3,2,1:T(8,128)S(1)}, f32[256,1,3,3,3,128]{5,0,4,3,2,1:T(8,128)}, u32[]{:S(2)}) copy-start(f32[256,1,3,3,3,128]{5,0,4,3,2,1:T(8,128)} %convolution_bitcast_fusion) | copy-start | bytes 10616836
  165.6 129.1 %copy-start.1 = (bf16[256,3,3,3,128]{4,0,3,2,1:T(8,128)(2,1)S(1)}, bf16[256,3,3,3,128]{4,0,3,2,1:T(8,128)(2,1)}, u32[]{:S(2)}) copy-start(bf16[256,3,3,3,128]{4,0,3,2,1:T(8,128)(2,1)} %param.10) | copy-start | bytes 5308420
Sparse Core Ops, SparseCore 0:
  35.3 7.4 reduce-scatter.3
  110.4 5.4 reduce-scatter.5
  165.7 126.8 reduce-scatter.7
